TPU v7x, 128 devices: a whole 4x4x4 slice. The times are simulated.
128 devices in a mesh: row: 8 (over x, core), col: 16 (over z, y).
Axes of the slice: x: 4, y: 4, z: 4, core: 2. Of those that a mesh axis runs over, the one named last changes fastest.
Arguments:
- kernel: bfloat16 [32768, 32768], P('row', 'col'), may hold values from -1 to 1
- random_cols: bfloat16 [32768, 256], P('row'), may hold values from -6 to 6
- tree_perm: int32 [32768], replicated, may hold values from 0 to 32767, as said below
- leaf_units: int32 [32], replicated, may hold values from 1 to 8, 160 in all
Outputs:
- bases: bfloat16 [4, 32768, 256], P(None, ('row', 'col'))
Inputs may be any that keep to these rules, and one draw needn't show every extreme that they name: `tree_perm`: A permutation. Cut tree positions and stored rows alike into blocks of 256 in order: every tree block takes at most 2 rows from any one stored block, some pair of blocks shares exactly 2, and every stored block gives 256 rows in all. `leaf_units`: they sum to 160.
All inputs are finite; a program needn't handle non-finite values.
Results may differ from a plain program's by a relative error of at most 0.0067.
Values may be sent and summed in bfloat16 or wider, within the bound.
No kernel may reach another device: no remote copies, remote signals or barrier semaphores. Data moves between devices by JAX's collectives and lax.ppermute only.
A program may use at most 192 MiB of HBM per device.

v0:
```python
import jax
import jax.numpy as jnp
from jax import lax
from jax.sharding import PartitionSpec as P

UNIT = 128
MINU = 4
LEVELS = 3


def shards(kernel, random_cols, tree_perm, leaf_units):
    width = random_cols.shape[1]
    partial_w = lax.dot_general(
        kernel, random_cols, (((0,), (0,)), ((), ())), preferred_element_type=jnp.float32
    )
    sample_w = lax.psum(partial_w, "row").astype(jnp.bfloat16)
    columns_count = lax.axis_size("col")
    rows_dev = kernel.shape[0] // columns_count
    sample = lax.psum_scatter(
        jnp.dot(kernel, sample_w, preferred_element_type=jnp.float32),
        "col",
        scatter_dimension=0,
        tiled=True,
    ).astype(jnp.bfloat16)
    total_rows = tree_perm.shape[0]
    device = lax.axis_index(("row", "col"))
    offset = device * rows_dev
    wanted = lax.dynamic_slice_in_dim(tree_perm, offset, rows_dev)
    inverse = (
        jnp.zeros((total_rows,), jnp.int32)
        .at[tree_perm]
        .set(jnp.arange(total_rows, dtype=jnp.int32))
    )
    placed = lax.dynamic_slice_in_dim(inverse, offset, rows_dev)
    everything = lax.all_gather(sample, ("row", "col"), axis=0, tiled=True)
    tree_rows = jnp.take(everything, wanted, axis=0)
    sizes = UNIT * (MINU - 1 + leaf_units)
    leaves = sizes.shape[0]
    ends = jnp.cumsum(sizes)
    positions = offset + jnp.arange(rows_dev, dtype=jnp.int32)
    leaf_of = jnp.sum(positions[:, None] >= ends[None, :], axis=1)
    reach = rows_dev // (UNIT * MINU) + 2
    offsets = jnp.arange(reach, dtype=jnp.int32)
    levels = LEVELS + 1
    node_ids = [leaf_of // 2**level for level in range(levels)]
    totals = []
    stored_leaf = jnp.sum(placed[:, None] >= ends[None, :], axis=1)
    leaf_range = jnp.arange(leaves, dtype=jnp.int32)
    chosen = stored_leaf[None, :] == leaf_range[:, None]
    masked = jnp.where(chosen[:, :, None], sample[None, :, :], jnp.zeros((), jnp.bfloat16))
    spread = jnp.einsum("lrs,rt->lst", masked, sample, preferred_element_type=jnp.float32)
    leaf_grams = lax.psum(spread, ("row", "col"))
    for level in range(levels):
        group = 2**level
        count = leaves // group
        node_grams = leaf_grams.reshape(count, group, width, width).sum(axis=1)
        index = jnp.minimum(node_ids[level][0] + offsets, count - 1)
        totals.append(jnp.take(node_grams, index, axis=0))
    identity_matrix = jnp.eye(width, dtype=jnp.float32)
    values = tree_rows.astype(jnp.float32).T
    results = []
    for level in range(levels):
        ids = node_ids[level]
        group = 2**level
        count = leaves // group
        node_sizes = sizes.reshape(count, group).sum(axis=1)
        candidate = ids[0] + offsets
        present = candidate <= ids[-1]
        counts = jnp.take(node_sizes, jnp.minimum(candidate, count - 1)).astype(jnp.float32)
        mean = jnp.where(
            present[:, None, None], totals[level] / counts[:, None, None], identity_matrix[None]
        )
        factor = jnp.linalg.cholesky(mean)
        basis = jnp.zeros((rows_dev, width), jnp.float32)
        for which in range(reach):
            solved = jax.scipy.linalg.solve_triangular(factor[which], values, lower=True).T
            basis = basis + jnp.where((ids == candidate[which])[:, None], solved, 0.0)
        results.append(basis.astype(jnp.bfloat16))
    return jnp.stack(results)


def solution(mesh):
    return jax.shard_map(
        shards,
        mesh=mesh,
        in_specs=(P("row", "col"), P("row", None), P(), P()),
        out_specs=P(None, ("row", "col"), None),
        check_vma=False,
    )
```

profile of v0, /device:TPU:1, one launch (start us, length us, event | category | flops | bytes accessed | tf_op | source)
XLA Modules:
  0.0 931.9 jit_solution(916774655061557949)
XLA Ops:
  6.5 1.6 copy-done
  8.1 9.7 %fusion.100 = f32[2048,256]{1,0:T(8,128)} fusion(bf16[4096,2048]{1,0:T(8,128)(2,1)} %param.7, bf16[4096,256]{1,0:T(8,128)(2,1)S(1)} %copy-done), kind=kOutput, calls=%fused_computation.278 | convolution fusion | flops 4294967296 | bytes 20971520 | tf_op jit(solution)/shard_map/dot_general | solution.py:13
  17.8 52.9 %all-reduce.5 = bf16[2048,256]{1,0:T(8,128)(2,1)S(1)} all-reduce(f32[2048,256]{1,0:T(8,128)} %fusion.100), channel_id=1, replica_groups=mesh['row'=8,'col'=16] {'row'}, use_global_device_ids=true, to_apply=%region_4.5 | all-reduce | flops 524288 | bytes 3145728 | tf_op jit(solution)/shard_map/psum | solution.py:16
  70.7 10.1 %convolution_bitcast_fusion = f32[4096,256]{0,1:T(8,128)} fusion(bf16[4096,2048]{1,0:T(8,128)(2,1)} %param.7, bf16[2048,256]{1,0:T(8,128)(2,1)S(1)} %all-reduce.5), kind=kOutput, calls=%fused_computation.29 | convolution fusion | flops 4294967296 | bytes 22020096 | tf_op jit(solution)/shard_map/dot_general | solution.py:20
  81.9 120.1 %scatter_custom_fusion = s32[32768]{0:T(1024)S(1)} fusion(s32[32768]{0:T(1024)S(1)} %compare_select_fusion, s32[32768]{0:T(1024)S(1)} %iota.117, s32[]{:T(128)} %copy.139), kind=kCustom, calls=%fused_computation.181 | custom fusion | bytes 131076 | tf_op jit(solution)/shard_map/scatter | solution.py:32
  203.1 4.5 fusion
  207.7 12.0 %all-gather.2.cloned.1.call-start = ((), (), s32[]{:S(2)}) async-start(), calls=%async_computation.3 | async-start | bytes 16908288 | tf_op jit(solution)/shard_map/all_gather | solution.py:35
  231.2 1.3 compare_and_fusion
  232.6 1.3 compare_and_fusion.2
  233.9 2.5 broadcast_compare_fusion.9
  236.4 2.6 broadcast_compare_fusion.11
  245.2 1.4 select_convert_fusion
  246.6 1.7 broadcast_compare_fusion.5
  248.4 1.7 broadcast_compare_fusion.8
  250.1 3.1 broadcast_compare_fusion.1
  253.2 119.0 %all-reduce.4.cloned.1.call-done = f32[32,256,256]{2,1,0:T(8,128)} async-done(((f32[32,256,256]{2,1,0:T(8,128)}), f32[32,256,256]{2,1,0:T(8,128)}) %all-reduce.4.cloned.1.call-update) | async-done | bytes 8388624 | tf_op jit(solution)/shard_map/psum | solution.py:52
  372.1 4.2 bitcast_reduce_fusion.1
  377.2 6.5 bitcast_reduce_fusion.2
  383.7 2.9 gather_fusion.3
  386.7 4.1 bitcast_reduce_fusion
  392.4 4.0 gather_fusion
  397.4 1.5 divide_select_fusion.1
  400.0 23.5 %custom-call.29 = f32[2,128,128]{2,1,0:T(8,128)S(1)} custom-call(f32[2,128,128]{2,1,0:T(8,128)S(1)} %cholesky.350), custom_call_target="Cholesky" | custom-call | tf_op jit(solution)/shard_map/jit(cholesky)/cholesky | solution.py:73
  423.7 23.5 %custom-call.39 = f32[2,128,128]{2,1,0:T(8,128)S(1)} custom-call(f32[2,128,128]{2,1,0:T(8,128)S(1)} %cholesky.356), custom_call_target="Cholesky" | custom-call | tf_op jit(solution)/shard_map/jit(cholesky)/cholesky | solution.py:73
  448.3 23.5 %custom-call.34 = f32[2,128,128]{2,1,0:T(8,128)S(1)} custom-call(f32[2,128,128]{2,1,0:T(8,128)S(1)} %cholesky.353), custom_call_target="Cholesky" | custom-call | tf_op jit(solution)/shard_map/jit(cholesky)/cholesky | solution.py:73
  472.1 23.9 %custom-call.44 = f32[2,128,128]{2,1,0:T(8,128)S(1)} custom-call(f32[2,128,128]{2,1,0:T(8,128)S(1)} %cholesky.359), custom_call_target="Cholesky" | custom-call | tf_op jit(solution)/shard_map/jit(cholesky)/cholesky | solution.py:73
  496.0 1.5 select_bitcast_fusion.1
  497.4 19.7 %custom-call.30 = f32[2,1,128,128]{2,3,1,0:T(8,128)S(1)} custom-call(f32[2,1,128,128]{3,2,1,0:T(8,128)S(1)} %get-tuple-element.180), custom_call_target="InvertDiagBlocksLowerTriangular" | custom-call | tf_op jit(solution)/shard_map/jit(cholesky)/cholesky | solution.py:73
  517.8 23.5 %custom-call.31 = f32[2,128,128]{2,1,0:T(8,128)S(1)} custom-call(f32[2,128,128]{2,1,0:T(8,128)S(1)} %convolution_subtract_fusion.11), custom_call_target="Cholesky" | custom-call | tf_op jit(solution)/shard_map/jit(cholesky)/cholesky | solution.py:73
  541.3 19.8 %custom-call.35 = f32[2,1,128,128]{2,3,1,0:T(8,128)S(1)} custom-call(f32[2,1,128,128]{3,2,1,0:T(8,128)S(1)} %get-tuple-element.178), custom_call_target="InvertDiagBlocksLowerTriangular" | custom-call | tf_op jit(solution)/shard_map/jit(cholesky)/cholesky | solution.py:73
  563.7 23.5 %custom-call.36 = f32[2,128,128]{2,1,0:T(8,128)S(1)} custom-call(f32[2,128,128]{2,1,0:T(8,128)S(1)} %convolution_subtract_fusion.10), custom_call_target="Cholesky" | custom-call | tf_op jit(solution)/shard_map/jit(cholesky)/cholesky | solution.py:73
  587.2 21.1 %custom-call.40 = f32[2,1,128,128]{2,3,1,0:T(8,128)} custom-call(f32[2,1,128,128]{3,2,1,0:T(8,128)} %get-tuple-element.177), custom_call_target="InvertDiagBlocksLowerTriangular" | custom-call | tf_op jit(solution)/shard_map/jit(cholesky)/cholesky | solution.py:73
  610.5 25.1 %custom-call.41 = f32[2,128,128]{2,1,0:T(8,128)} custom-call(f32[2,128,128]{2,1,0:T(8,128)} %convolution_subtract_fusion.9), custom_call_target="Cholesky" | custom-call | tf_op jit(solution)/shard_map/jit(cholesky)/cholesky | solution.py:73
  636.5 21.1 %custom-call.45 = f32[2,1,128,128]{2,3,1,0:T(8,128)} custom-call(f32[2,1,128,128]{3,2,1,0:T(8,128)} %get-tuple-element.179), custom_call_target="InvertDiagBlocksLowerTriangular" | custom-call | tf_op jit(solution)/shard_map/jit(cholesky)/cholesky | solution.py:73
  659.9 24.3 %custom-call.46 = f32[2,128,128]{2,1,0:T(8,128)S(1)} custom-call(f32[2,128,128]{2,1,0:T(8,128)} %convolution_subtract_fusion.8), custom_call_target="Cholesky" | custom-call | tf_op jit(solution)/shard_map/jit(cholesky)/cholesky | solution.py:73
  686.2 1.5 select_select_fusion.3
  688.4 3.8 while.23
  692.3 20.1 %custom-call.48 = f32[2,128,128]{1,2,0:T(8,128)S(1)} custom-call(f32[2,128,128]{2,1,0:T(8,128)S(1)} %get-tuple-element.64), custom_call_target="InvertDiagBlocksLowerTriangular" | custom-call | tf_op jit(solution)/shard_map/jit(_solve_triangular)/triangular_solve | solution.py:76
  712.4 4.0 while.22
  713.0 1.4 bitcast_dynamic-update-slice_fusion.22
  715.0 1.4 bitcast_dynamic-update-slice_fusion.22
  716.4 20.3 %custom-call.47 = f32[2,128,128]{1,2,0:T(8,128)} custom-call(f32[2,128,128]{2,1,0:T(8,128)S(1)} %get-tuple-element.63), custom_call_target="InvertDiagBlocksLowerTriangular" | custom-call | tf_op jit(solution)/shard_map/jit(_solve_triangular)/triangular_solve | solution.py:76
  736.7 4.1 while.21
  737.3 1.4 bitcast_dynamic-update-slice_fusion.21
  739.4 1.4 bitcast_dynamic-update-slice_fusion.21
  740.8 19.7 %custom-call.43 = f32[2,128,128]{1,2,0:T(8,128)S(1)} custom-call(f32[2,128,128]{2,1,0:T(8,128)S(1)} %get-tuple-element.62), custom_call_target="InvertDiagBlocksLowerTriangular" | custom-call | tf_op jit(solution)/shard_map/jit(_solve_triangular)/triangular_solve | solution.py:76
  760.5 3.9 while.20
  761.1 1.4 bitcast_dynamic-update-slice_fusion.20
  763.1 1.4 bitcast_dynamic-update-slice_fusion.20
  764.5 19.7 %custom-call.42 = f32[2,128,128]{1,2,0:T(8,128)S(1)} custom-call(f32[2,128,128]{2,1,0:T(8,128)S(1)} %get-tuple-element.61), custom_call_target="InvertDiagBlocksLowerTriangular" | custom-call | tf_op jit(solution)/shard_map/jit(_solve_triangular)/triangular_solve | solution.py:76
  784.2 3.9 while.19
  784.8 1.3 bitcast_dynamic-update-slice_fusion.19
  786.7 1.3 bitcast_dynamic-update-slice_fusion.19
  788.1 19.7 %custom-call.38 = f32[2,128,128]{1,2,0:T(8,128)S(1)} custom-call(f32[2,128,128]{2,1,0:T(8,128)S(1)} %get-tuple-element.60), custom_call_target="InvertDiagBlocksLowerTriangular" | custom-call | tf_op jit(solution)/shard_map/jit(_solve_triangular)/triangular_solve | solution.py:76
  807.8 4.0 while.18
  808.4 1.4 bitcast_dynamic-update-slice_fusion.18
  810.4 1.4 bitcast_dynamic-update-slice_fusion.18
  811.7 20.5 %custom-call.37 = f32[2,128,128]{1,2,0:T(8,128)} custom-call(f32[2,128,128]{2,1,0:T(8,128)S(1)} %get-tuple-element.59), custom_call_target="InvertDiagBlocksLowerTriangular" | custom-call | tf_op jit(solution)/shard_map/jit(_solve_triangular)/triangular_solve | solution.py:76
  832.3 3.8 while.17
  836.1 20.3 %custom-call.33 = f32[2,128,128]{1,2,0:T(8,128)} custom-call(f32[2,128,128]{2,1,0:T(8,128)S(1)} %get-tuple-element.58), custom_call_target="InvertDiagBlocksLowerTriangular" | custom-call | tf_op jit(solution)/shard_map/jit(_solve_triangular)/triangular_solve | solution.py:76
  856.4 3.6 while.16
  860.0 20.3 %custom-call.32 = f32[2,128,128]{1,2,0:T(8,128)} custom-call(f32[2,128,128]{2,1,0:T(8,128)S(1)} %get-tuple-element.57), custom_call_target="InvertDiagBlocksLowerTriangular" | custom-call | tf_op jit(solution)/shard_map/jit(_solve_triangular)/triangular_solve | solution.py:76
  880.3 22.6 %copy.47 = bf16[32768,256]{1,0:T(8,128)(2,1)} copy(bf16[32768,256]{0,1:T(8,128)(2,1)} %all-gather.2.cloned.1.call-done) | data formatting | bytes 33554432 | tf_op jit(solution)/shard_map/all_gather | solution.py:35
  902.9 9.0 gather_fusion.2
  (234 shorter events, 67.4 us)
Async XLA Ops:
  6.5 1.6 copy-start
  6.5 195.6 %reduce-scatter.2.cloned.1.call-start = ((), (), s32[]{:S(2)}) async-start(), calls=%async_computation.1 | async-start | bytes 4456448 | tf_op jit(solution)/shard_map/reduce_scatter | solution.py:19
  80.9 0.7 copy-start.25
  80.9 0.9 copy-start.11
  80.9 291.2 %all-reduce.4.cloned.1.call-start = ((), (), s32[]{:S(2)}) async-start(), calls=%async_computation.2 | async-start | bytes 16777216 | tf_op jit(solution)/shard_map/psum | solution.py:52
  203.1 4.5 copy-start.2
  207.7 672.6 %all-gather.2.cloned.1.call-start = ((), (), s32[]{:S(2)}) async-start(), calls=%async_computation.3 | async-start | bytes 16908288 | tf_op jit(solution)/shard_map/all_gather | solution.py:35
  399.2 0.8 copy-start.6
  423.7 93.4 %copy-start.7 = (f32[2,256,256]{2,1,0:T(8,128)S(1)}, f32[2,256,256]{2,1,0:T(8,128)}, u32[]{:S(2)}) copy-start(f32[2,256,256]{2,1,0:T(8,128)} %copy-done.6) | copy-start | bytes 1572868
  447.5 0.8 copy-start.8
  495.9 1.5 copy-start.9
  517.8 166.3 %copy-start.10 = (f32[2,128,128]{2,1,0:T(8,128)S(1)}, f32[2,128,128]{2,1,0:T(8,128)}, u32[]{:S(2)}) copy-start(f32[2,128,128]{2,1,0:T(8,128)} %copy-done.9) | copy-start | bytes 393220
  685.1 1.0 copy-start.3
  685.2 1.0 copy-start.4
  807.8 108.1 %copy-start.13 = (f32[2,128,128]{1,2,0:T(8,128)}, f32[2,128,128]{1,2,0:T(8,128)S(1)}, u32[]{:S(2)}) copy-start(f32[2,128,128]{1,2,0:T(8,128)S(1)} %custom-call.38) | copy-start | bytes 393220
  836.1 66.9 %copy-start.5 = (f32[256,256]{1,0:T(8,128)}, f32[256,256]{1,0:T(8,128)S(1)}, u32[]{:S(2)}) copy-start(f32[256,256]{1,0:T(8,128)S(1)} %get-tuple-element.602) | copy-start | bytes 786436
  880.3 31.8 %copy-start.24 = (pred[256]{0:T(512)(128)(4,1)S(1)}, pred[256]{0:T(512)(128)(4,1)}, u32[]{:S(2)}) copy-start(pred[256]{0:T(512)(128)(4,1)} %get-tuple-element.139) | copy-start | bytes 772
  880.3 32.8 %copy-start.12 = (f32[2,128,128]{1,2,0:T(8,128)S(1)}, f32[2,128,128]{1,2,0:T(8,128)}, u32[]{:S(2)}) copy-start(f32[2,128,128]{1,2,0:T(8,128)} %custom-call.47) | copy-start | bytes 393220
  912.1 10.5 %copy-start.14 = (f32[2,128,128]{1,2,0:T(8,128)S(1)}, f32[2,128,128]{1,2,0:T(8,128)}, u32[]{:S(2)}) copy-start(f32[2,128,128]{1,2,0:T(8,128)} %custom-call.33) | copy-start | bytes 393220
  912.1 10.8 %copy-start.15 = (f32[2,128,128]{1,2,0:T(8,128)S(1)}, f32[2,128,128]{1,2,0:T(8,128)}, u32[]{:S(2)}) copy-start(f32[2,128,128]{1,2,0:T(8,128)} %custom-call.32) | copy-start | bytes 393220
  912.4 11.4 %copy-start.18 = (pred[256]{0:T(512)(128)(4,1)S(1)}, pred[256]{0:T(512)(128)(4,1)}, u32[]{:S(2)}) copy-start(pred[256]{0:T(512)(128)(4,1)} %get-tuple-element.187) | copy-start | bytes 772
  912.5 11.4 %copy-start.19 = (pred[256]{0:T(512)(128)(4,1)S(1)}, pred[256]{0:T(512)(128)(4,1)}, u32[]{:S(2)}) copy-start(pred[256]{0:T(512)(128)(4,1)} %get-tuple-element.188) | copy-start | bytes 772
  913.1 10.8 %copy-start.16 = (pred[256]{0:T(512)(128)(4,1)S(1)}, pred[256]{0:T(512)(128)(4,1)}, u32[]{:S(2)}) copy-start(pred[256]{0:T(512)(128)(4,1)} %get-tuple-element.226) | copy-start | bytes 772
  913.1 10.8 %copy-start.17 = (pred[256]{0:T(512)(128)(4,1)S(1)}, pred[256]{0:T(512)(128)(4,1)}, u32[]{:S(2)}) copy-start(pred[256]{0:T(512)(128)(4,1)} %get-tuple-element.227) | copy-start | bytes 772
  913.7 10.3 %copy-start.22 = (pred[256]{0:T(512)(128)(4,1)S(1)}, pred[256]{0:T(512)(128)(4,1)}, u32[]{:S(2)}) copy-start(pred[256]{0:T(512)(128)(4,1)} %get-tuple-element.183) | copy-start | bytes 772
  913.7 10.3 %copy-start.23 = (pred[256]{0:T(512)(128)(4,1)S(1)}, pred[256]{0:T(512)(128)(4,1)}, u32[]{:S(2)}) copy-start(pred[256]{0:T(512)(128)(4,1)} %get-tuple-element.184) | copy-start | bytes 772
  914.3 9.7 %copy-start.20 = (pred[256]{0:T(512)(128)(4,1)S(1)}, pred[256]{0:T(512)(128)(4,1)}, u32[]{:S(2)}) copy-start(pred[256]{0:T(512)(128)(4,1)} %get-tuple-element.181) | copy-start | bytes 772
  914.3 9.7 %copy-start.21 = (pred[256]{0:T(512)(128)(4,1)S(1)}, pred[256]{0:T(512)(128)(4,1)}, u32[]{:S(2)}) copy-start(pred[256]{0:T(512)(128)(4,1)} %get-tuple-element.182) | copy-start | bytes 772
  916.2 9.0 copy-start.1
Sparse Core Ops, SparseCore 0:
  81.0 79.6 reduce-scatter.1
  207.8 164.3 all-reduce.3
  375.0 98.1 all-gather.1
where the time goes:
time: 940 us; the launch traced here: 932 us
  other arithmetic  481 us (51%)
  local copies, waits for them, and re-layouts  208 us (22%)
  waiting for transfers between devices  119 us (13%)
  blocking collectives  52.9 us (6%)
  matrix products  43.3 us (5%)
  between operations  14.6 us (2%)
  starting transfers between devices  12 us (1%)
    another operation x28, other arithmetic, shards(): factor = jnp.linalg.cholesky(mean)  276 us
    another operation x14, other arithmetic, shards(): jax.scipy.linalg.solve_triangular(factor[which], values, lower=True)  162 us
    scatter x1, local copies, waits for them, and re-layouts, shards(): inverse = jnp.zeros((total_rows,), jnp.int32).at[tree_perm].set(jnp.arang...  120 us
    psum x1, waiting for transfers between devices, shards(): leaf_grams = lax.psum(spread, ('row', 'col'))  119 us
    psum x1, blocking collectives, shards(): sample_w = lax.psum(partial_w, 'row').astype(jnp.bfloat16)  52.9 us
    another operation x49, local copies, waits for them, and re-layouts, shards(): jax.scipy.linalg.solve_triangular(factor[which], values, lower=True)  31.3 us
    all_gather x1, local copies, waits for them, and re-layouts, shards(): everything = lax.all_gather(sample, ('row', 'col'), axis=0, tiled=True)  22.6 us
  transfers between devices with their start and end apart: 3, of which 1 were waited for; matrix products, arithmetic and copies ran while one was open for 71% of the time, Pallas kernels for 0%

commit v1 on v0

--- a/solution.py
+++ b/solution.py
@@ -49,7 +49,7 @@
     chosen = stored_leaf[None, :] == leaf_range[:, None]
     masked = jnp.where(chosen[:, :, None], sample[None, :, :], jnp.zeros((), jnp.bfloat16))
     spread = jnp.einsum("lrs,rt->lst", masked, sample, preferred_element_type=jnp.float32)
-    leaf_grams = lax.psum(spread, ("row", "col"))
+    leaf_grams = lax.psum(lax.psum(spread, "col"), "row")
     for level in range(levels):
         group = 2**level
         count = leaves // group

time: 940 us -> 1030 us (1.096)
  waiting for transfers between devices: 119 us -> 204 us
    psum x1 -> x2, waiting for transfers between devices: 119 us -> 204 us  [shards(): leaf_grams = lax.psum(lax.psum(spread, 'col'), 'row')]
  transfers between devices with their start and end apart: 3 -> 4, of which waited for: 1 -> 2; matrix products, arithmetic and copies ran while one was open for 71% -> 65% of each run, Pallas kernels for 0% -> 0%
where the time goes in v1:
time: 1030 us; the launch traced here: 1020 us
  other arithmetic  481 us (47%)
  local copies, waits for them, and re-layouts  208 us (20%)
  waiting for transfers between devices  204 us (20%)
  blocking collectives  52.9 us (5%)
  matrix products  43.3 us (4%)
  between operations  14.6 us (1%)
  starting transfers between devices  12.1 us (1%)
    another operation x28, other arithmetic, shards(): factor = jnp.linalg.cholesky(mean)  276 us
    psum x2, waiting for transfers between devices, shards(): leaf_grams = lax.psum(lax.psum(spread, 'col'), 'row')  204 us
    another operation x14, other arithmetic, shards(): jax.scipy.linalg.solve_triangular(factor[which], values, lower=True)  162 us
    scatter x1, local copies, waits for them, and re-layouts, shards(): inverse = jnp.zeros((total_rows,), jnp.int32).at[tree_perm].set(jnp.arang...  120 us
    psum x1, blocking collectives, shards(): sample_w = lax.psum(partial_w, 'row').astype(jnp.bfloat16)  52.9 us
    another operation x49, local copies, waits for them, and re-layouts, shards(): jax.scipy.linalg.solve_triangular(factor[which], values, lower=True)  31.3 us
    all_gather x1, local copies, waits for them, and re-layouts, shards(): everything = lax.all_gather(sample, ('row', 'col'), axis=0, tiled=True)  22.6 us
  transfers between devices with their start and end apart: 4, of which 2 were waited for; matrix products, arithmetic and copies ran while one was open for 65% of the time, Pallas kernels for 0%

profile of v1, /device:TPU:1, one launch (start us, length us, event | category | flops | bytes accessed | tf_op | source)
XLA Modules:
  0.0 1017.3 jit_solution(11663155272117724596)
XLA Ops:
  6.5 1.6 copy-done
  8.1 9.7 fusion.100
  17.8 52.9 %all-reduce.8 = bf16[2048,256]{1,0:T(8,128)(2,1)S(1)} all-reduce(f32[2048,256]{1,0:T(8,128)} %fusion.100), channel_id=1, replica_groups=mesh['row'=8,'col'=16] {'row'}, use_global_device_ids=true, to_apply=%region_4.5 | all-reduce | flops 524288 | bytes 3145728 | tf_op jit(solution)/shard_map/psum | solution.py:16
  70.7 10.1 convolution_bitcast_fusion
  81.9 120.1 %scatter_custom_fusion = s32[32768]{0:T(1024)S(1)} fusion(s32[32768]{0:T(1024)S(1)} %compare_select_fusion, s32[32768]{0:T(1024)S(1)} %iota.117, s32[]{:T(128)} %copy.140), kind=kCustom, calls=%fused_computation.181 | custom fusion | bytes 131076 | tf_op jit(solution)/shard_map/scatter | solution.py:32
  203.1 4.5 fusion
  207.7 144.4 %all-reduce.5.cloned.1.call-done = f32[32,256,256]{2,1,0:T(8,128)} async-done(((f32[32,256,256]{2,1,0:T(8,128)}), f32[32,256,256]{2,1,0:T(8,128)}) %all-reduce.5.cloned.1.call-update) | async-done | bytes 8388624 | tf_op jit(solution)/shard_map/psum | solution.py:52
  352.1 12.0 %all-gather.2.cloned.1.call-start = ((), (), s32[]{:S(2)}) async-start(), calls=%async_computation.4 | async-start | bytes 16908288 | tf_op jit(solution)/shard_map/all_gather | solution.py:35
  366.0 1.3 fusion.78
  369.2 1.3 fusion.80
  375.7 1.3 compare_and_fusion
  377.0 1.3 compare_and_fusion.2
  378.3 2.6 broadcast_compare_fusion.9
  380.9 2.5 broadcast_compare_fusion.11
  391.1 1.7 broadcast_compare_fusion.5
  392.8 1.7 broadcast_compare_fusion.8
  394.5 3.1 broadcast_compare_fusion.1
  397.6 60.0 %all-reduce.7.cloned.1.call-done = f32[32,256,256]{2,1,0:T(8,128)} async-done(((f32[32,256,256]{2,1,0:T(8,128)}), f32[32,256,256]{2,1,0:T(8,128)}) %all-reduce.7.cloned.1.call-update) | async-done | bytes 8388624 | tf_op jit(solution)/shard_map/psum | solution.py:52
  457.6 4.2 bitcast_reduce_fusion.1
  462.6 6.5 bitcast_reduce_fusion.2
  469.1 2.8 gather_fusion.3
  472.1 4.1 bitcast_reduce_fusion
  477.8 4.0 gather_fusion
  482.8 1.5 divide_select_fusion.1
  485.4 23.5 %custom-call.29 = f32[2,128,128]{2,1,0:T(8,128)S(1)} custom-call(f32[2,128,128]{2,1,0:T(8,128)S(1)} %cholesky.350), custom_call_target="Cholesky" | custom-call | tf_op jit(solution)/shard_map/jit(cholesky)/cholesky | solution.py:73
  509.2 23.5 %custom-call.39 = f32[2,128,128]{2,1,0:T(8,128)S(1)} custom-call(f32[2,128,128]{2,1,0:T(8,128)S(1)} %cholesky.356), custom_call_target="Cholesky" | custom-call | tf_op jit(solution)/shard_map/jit(cholesky)/cholesky | solution.py:73
  533.7 23.5 %custom-call.34 = f32[2,128,128]{2,1,0:T(8,128)S(1)} custom-call(f32[2,128,128]{2,1,0:T(8,128)S(1)} %cholesky.353), custom_call_target="Cholesky" | custom-call | tf_op jit(solution)/shard_map/jit(cholesky)/cholesky | solution.py:73
  557.5 23.9 %custom-call.44 = f32[2,128,128]{2,1,0:T(8,128)S(1)} custom-call(f32[2,128,128]{2,1,0:T(8,128)S(1)} %cholesky.359), custom_call_target="Cholesky" | custom-call | tf_op jit(solution)/shard_map/jit(cholesky)/cholesky | solution.py:73
  581.4 1.5 select_bitcast_fusion.1
  582.9 19.7 %custom-call.30 = f32[2,1,128,128]{2,3,1,0:T(8,128)S(1)} custom-call(f32[2,1,128,128]{3,2,1,0:T(8,128)S(1)} %get-tuple-element.180), custom_call_target="InvertDiagBlocksLowerTriangular" | custom-call | tf_op jit(solution)/shard_map/jit(cholesky)/cholesky | solution.py:73
  603.2 23.5 %custom-call.31 = f32[2,128,128]{2,1,0:T(8,128)S(1)} custom-call(f32[2,128,128]{2,1,0:T(8,128)S(1)} %convolution_subtract_fusion.11), custom_call_target="Cholesky" | custom-call | tf_op jit(solution)/shard_map/jit(cholesky)/cholesky | solution.py:73
  626.7 19.8 %custom-call.35 = f32[2,1,128,128]{2,3,1,0:T(8,128)S(1)} custom-call(f32[2,1,128,128]{3,2,1,0:T(8,128)S(1)} %get-tuple-element.178), custom_call_target="InvertDiagBlocksLowerTriangular" | custom-call | tf_op jit(solution)/shard_map/jit(cholesky)/cholesky | solution.py:73
  649.1 23.5 %custom-call.36 = f32[2,128,128]{2,1,0:T(8,128)S(1)} custom-call(f32[2,128,128]{2,1,0:T(8,128)S(1)} %convolution_subtract_fusion.10), custom_call_target="Cholesky" | custom-call | tf_op jit(solution)/shard_map/jit(cholesky)/cholesky | solution.py:73
  672.6 21.1 %custom-call.40 = f32[2,1,128,128]{2,3,1,0:T(8,128)} custom-call(f32[2,1,128,128]{3,2,1,0:T(8,128)} %get-tuple-element.177), custom_call_target="InvertDiagBlocksLowerTriangular" | custom-call | tf_op jit(solution)/shard_map/jit(cholesky)/cholesky | solution.py:73
  695.9 25.1 %custom-call.41 = f32[2,128,128]{2,1,0:T(8,128)} custom-call(f32[2,128,128]{2,1,0:T(8,128)} %convolution_subtract_fusion.9), custom_call_target="Cholesky" | custom-call | tf_op jit(solution)/shard_map/jit(cholesky)/cholesky | solution.py:73
  721.9 21.1 %custom-call.45 = f32[2,1,128,128]{2,3,1,0:T(8,128)} custom-call(f32[2,1,128,128]{3,2,1,0:T(8,128)} %get-tuple-element.179), custom_call_target="InvertDiagBlocksLowerTriangular" | custom-call | tf_op jit(solution)/shard_map/jit(cholesky)/cholesky | solution.py:73
  745.3 24.3 %custom-call.46 = f32[2,128,128]{2,1,0:T(8,128)S(1)} custom-call(f32[2,128,128]{2,1,0:T(8,128)} %convolution_subtract_fusion.8), custom_call_target="Cholesky" | custom-call | tf_op jit(solution)/shard_map/jit(cholesky)/cholesky | solution.py:73
  771.6 1.5 select_select_fusion.3
  773.9 3.8 while.23
  777.7 20.1 %custom-call.48 = f32[2,128,128]{1,2,0:T(8,128)S(1)} custom-call(f32[2,128,128]{2,1,0:T(8,128)S(1)} %get-tuple-element.64), custom_call_target="InvertDiagBlocksLowerTriangular" | custom-call | tf_op jit(solution)/shard_map/jit(_solve_triangular)/triangular_solve | solution.py:76
  797.8 4.0 while.22
  798.4 1.4 bitcast_dynamic-update-slice_fusion.22
  800.4 1.4 bitcast_dynamic-update-slice_fusion.22
  801.8 20.3 %custom-call.47 = f32[2,128,128]{1,2,0:T(8,128)} custom-call(f32[2,128,128]{2,1,0:T(8,128)S(1)} %get-tuple-element.63), custom_call_target="InvertDiagBlocksLowerTriangular" | custom-call | tf_op jit(solution)/shard_map/jit(_solve_triangular)/triangular_solve | solution.py:76
  822.1 4.1 while.21
  822.7 1.4 bitcast_dynamic-update-slice_fusion.21
  824.8 1.4 bitcast_dynamic-update-slice_fusion.21
  826.2 19.7 %custom-call.43 = f32[2,128,128]{1,2,0:T(8,128)S(1)} custom-call(f32[2,128,128]{2,1,0:T(8,128)S(1)} %get-tuple-element.62), custom_call_target="InvertDiagBlocksLowerTriangular" | custom-call | tf_op jit(solution)/shard_map/jit(_solve_triangular)/triangular_solve | solution.py:76
  845.9 3.9 while.20
  846.5 1.4 bitcast_dynamic-update-slice_fusion.20
  848.5 1.4 bitcast_dynamic-update-slice_fusion.20
  849.9 19.7 %custom-call.42 = f32[2,128,128]{1,2,0:T(8,128)S(1)} custom-call(f32[2,128,128]{2,1,0:T(8,128)S(1)} %get-tuple-element.61), custom_call_target="InvertDiagBlocksLowerTriangular" | custom-call | tf_op jit(solution)/shard_map/jit(_solve_triangular)/triangular_solve | solution.py:76
  869.6 3.9 while.19
  873.5 19.7 %custom-call.38 = f32[2,128,128]{1,2,0:T(8,128)S(1)} custom-call(f32[2,128,128]{2,1,0:T(8,128)S(1)} %get-tuple-element.60), custom_call_target="InvertDiagBlocksLowerTriangular" | custom-call | tf_op jit(solution)/shard_map/jit(_solve_triangular)/triangular_solve | solution.py:76
  893.2 4.0 while.18
  893.8 1.4 bitcast_dynamic-update-slice_fusion.18
  895.8 1.4 bitcast_dynamic-update-slice_fusion.18
  897.2 20.5 %custom-call.37 = f32[2,128,128]{1,2,0:T(8,128)} custom-call(f32[2,128,128]{2,1,0:T(8,128)S(1)} %get-tuple-element.59), custom_call_target="InvertDiagBlocksLowerTriangular" | custom-call | tf_op jit(solution)/shard_map/jit(_solve_triangular)/triangular_solve | solution.py:76
  917.7 3.8 while.17
  921.5 20.3 %custom-call.33 = f32[2,128,128]{1,2,0:T(8,128)} custom-call(f32[2,128,128]{2,1,0:T(8,128)S(1)} %get-tuple-element.58), custom_call_target="InvertDiagBlocksLowerTriangular" | custom-call | tf_op jit(solution)/shard_map/jit(_solve_triangular)/triangular_solve | solution.py:76
  941.8 3.6 while.16
  945.4 20.3 %custom-call.32 = f32[2,128,128]{1,2,0:T(8,128)} custom-call(f32[2,128,128]{2,1,0:T(8,128)S(1)} %get-tuple-element.57), custom_call_target="InvertDiagBlocksLowerTriangular" | custom-call | tf_op jit(solution)/shard_map/jit(_solve_triangular)/triangular_solve | solution.py:76
  965.7 22.6 %copy.47 = bf16[32768,256]{1,0:T(8,128)(2,1)} copy(bf16[32768,256]{0,1:T(8,128)(2,1)} %all-gather.2.cloned.1.call-done) | data formatting | bytes 33554432 | tf_op jit(solution)/shard_map/all_gather | solution.py:35
  988.3 9.0 gather_fusion.2
  (237 shorter events, 68.8 us)
Async XLA Ops:
  6.5 1.6 copy-start
  6.5 195.6 %reduce-scatter.2.cloned.1.call-start = ((), (), s32[]{:S(2)}) async-start(), calls=%async_computation.1 | async-start | bytes 4456448 | tf_op jit(solution)/shard_map/reduce_scatter | solution.py:19
  80.9 0.7 copy-start.25
  80.9 0.9 copy-start.11
  80.9 271.2 %all-reduce.5.cloned.1.call-start = ((), (), s32[]{:S(2)}) async-start(), calls=%async_computation.2 | async-start | bytes 16777216 | tf_op jit(solution)/shard_map/psum | solution.py:52
  203.1 4.5 copy-start.2
  207.7 249.9 %all-reduce.7.cloned.1.call-start = ((), (), s32[]{:S(2)}) async-start(), calls=%async_computation.3 | async-start | bytes 16777216 | tf_op jit(solution)/shard_map/psum | solution.py:52
  352.1 613.6 %all-gather.2.cloned.1.call-start = ((), (), s32[]{:S(2)}) async-start(), calls=%async_computation.4 | async-start | bytes 16908288 | tf_op jit(solution)/shard_map/all_gather | solution.py:35
  484.6 0.8 copy-start.6
  509.1 93.4 %copy-start.7 = (f32[2,256,256]{2,1,0:T(8,128)S(1)}, f32[2,256,256]{2,1,0:T(8,128)}, u32[]{:S(2)}) copy-start(f32[2,256,256]{2,1,0:T(8,128)} %copy-done.6) | copy-start | bytes 1572868
  532.9 0.8 copy-start.8
  581.3 1.5 copy-start.9
  603.2 166.3 %copy-start.10 = (f32[2,128,128]{2,1,0:T(8,128)S(1)}, f32[2,128,128]{2,1,0:T(8,128)}, u32[]{:S(2)}) copy-start(f32[2,128,128]{2,1,0:T(8,128)} %copy-done.9) | copy-start | bytes 393220
  770.6 1.0 copy-start.3
  770.6 1.0 copy-start.4
  893.2 108.1 %copy-start.13 = (f32[2,128,128]{1,2,0:T(8,128)}, f32[2,128,128]{1,2,0:T(8,128)S(1)}, u32[]{:S(2)}) copy-start(f32[2,128,128]{1,2,0:T(8,128)S(1)} %custom-call.38) | copy-start | bytes 393220
  921.5 66.9 %copy-start.5 = (f32[256,256]{1,0:T(8,128)}, f32[256,256]{1,0:T(8,128)S(1)}, u32[]{:S(2)}) copy-start(f32[256,256]{1,0:T(8,128)S(1)} %get-tuple-element.606) | copy-start | bytes 786436
  965.7 31.8 %copy-start.24 = (pred[256]{0:T(512)(128)(4,1)S(1)}, pred[256]{0:T(512)(128)(4,1)}, u32[]{:S(2)}) copy-start(pred[256]{0:T(512)(128)(4,1)} %get-tuple-element.139) | copy-start | bytes 772
  965.7 32.8 %copy-start.12 = (f32[2,128,128]{1,2,0:T(8,128)S(1)}, f32[2,128,128]{1,2,0:T(8,128)}, u32[]{:S(2)}) copy-start(f32[2,128,128]{1,2,0:T(8,128)} %custom-call.47) | copy-start | bytes 393220
  997.5 10.5 %copy-start.14 = (f32[2,128,128]{1,2,0:T(8,128)S(1)}, f32[2,128,128]{1,2,0:T(8,128)}, u32[]{:S(2)}) copy-start(f32[2,128,128]{1,2,0:T(8,128)} %custom-call.33) | copy-start | bytes 393220
  997.5 10.8 %copy-start.15 = (f32[2,128,128]{1,2,0:T(8,128)S(1)}, f32[2,128,128]{1,2,0:T(8,128)}, u32[]{:S(2)}) copy-start(f32[2,128,128]{1,2,0:T(8,128)} %custom-call.32) | copy-start | bytes 393220
  997.9 11.4 %copy-start.18 = (pred[256]{0:T(512)(128)(4,1)S(1)}, pred[256]{0:T(512)(128)(4,1)}, u32[]{:S(2)}) copy-start(pred[256]{0:T(512)(128)(4,1)} %get-tuple-element.187) | copy-start | bytes 772
  997.9 11.4 %copy-start.19 = (pred[256]{0:T(512)(128)(4,1)S(1)}, pred[256]{0:T(512)(128)(4,1)}, u32[]{:S(2)}) copy-start(pred[256]{0:T(512)(128)(4,1)} %get-tuple-element.188) | copy-start | bytes 772
  998.5 10.8 %copy-start.16 = (pred[256]{0:T(512)(128)(4,1)S(1)}, pred[256]{0:T(512)(128)(4,1)}, u32[]{:S(2)}) copy-start(pred[256]{0:T(512)(128)(4,1)} %get-tuple-element.226) | copy-start | bytes 772
  998.5 10.8 %copy-start.17 = (pred[256]{0:T(512)(128)(4,1)S(1)}, pred[256]{0:T(512)(128)(4,1)}, u32[]{:S(2)}) copy-start(pred[256]{0:T(512)(128)(4,1)} %get-tuple-element.227) | copy-start | bytes 772
  999.1 10.3 %copy-start.22 = (pred[256]{0:T(512)(128)(4,1)S(1)}, pred[256]{0:T(512)(128)(4,1)}, u32[]{:S(2)}) copy-start(pred[256]{0:T(512)(128)(4,1)} %get-tuple-element.183) | copy-start | bytes 772
  999.1 10.3 %copy-start.23 = (pred[256]{0:T(512)(128)(4,1)S(1)}, pred[256]{0:T(512)(128)(4,1)}, u32[]{:S(2)}) copy-start(pred[256]{0:T(512)(128)(4,1)} %get-tuple-element.184) | copy-start | bytes 772
  999.7 9.7 copy-start.20
  999.7 9.7 copy-start.21
  1001.6 9.0 copy-start.1
Sparse Core Ops, SparseCore 0:
  81.0 79.6 reduce-scatter.1
  207.8 144.2 all-reduce.4
  354.5 103.0 all-reduce.6
  460.3 99.6 all-gather.1
